TPU v7x, 128 devices: a whole 4x4x4 slice. The times are simulated.
128 devices in a mesh: ep: 128 (over y, z, x, core).
Axes of the slice: x: 4, y: 4, z: 4, core: 2. Of those that a mesh axis runs over, the one named last changes fastest.
Arguments:
- tokens: bfloat16 [16384, 7168], P('ep'), may hold values from -6 to 6
- expert_ids: int32 [16384, 8], P('ep'), may hold values from 0 to 255, all different within a row; in each aligned block of 128 rows (0 to 127, 128 to 255, ...) at most 6 rows name the same one
Outputs:
- merged: bfloat16 [256, 768, 7168], P('ep')
- totals: int32 [256], P('ep')
Inputs may be any that keep to these rules, and one draw needn't show every extreme that they name: `expert_ids`: each row names 8 different experts; among the rows of one device (aligned blocks of 128 rows) no expert is named more than 6 times, a bound that some block reaches.
All inputs are finite; a program needn't handle non-finite values.
Results may differ from a plain program's by a relative error of at most 0.001.
Values may be sent and summed in bfloat16 or wider, within the bound.
A program may use at most 256 MiB of HBM per device.

v0:
```python
import jax
import jax.numpy as jnp
from jax import lax
from jax.sharding import PartitionSpec as P

EXPERTS = 256
CAP = 6


def side_by_side(arrays, axis, split_dim, concat_dim, along):
    columns = [a.reshape(*a.shape[:along], -1) for a in arrays]
    both = jnp.concatenate(columns, axis=along)
    result, at, gathered = (
        lax.all_to_all(both, axis, split_axis=split_dim, concat_axis=concat_dim, tiled=True),
        0,
        [],
    )
    for a, column in zip(arrays, columns):
        piece = result[..., at : at + column.shape[along]]
        gathered.append(piece.reshape(*piece.shape[:along], *a.shape[along:]))
        at += column.shape[along]
    return tuple(gathered)


def place_table(counts_int, capacity):
    owners = counts_int.shape[0]
    offsets = jnp.cumsum(counts_int, axis=0) - counts_int
    slot_index = jnp.arange(capacity, dtype=jnp.int32)
    filled = slot_index[None, None, :] < counts_int[:, :, None]
    target = offsets[:, :, None] + slot_index[None, None, :]
    line_index = jnp.arange(owners * capacity, dtype=jnp.int32)
    placer = (filled[None] & (target[None] == line_index[:, None, None, None])).astype(jnp.bfloat16)
    return placer


def compact(pieces):
    payload, arrived_counts = pieces
    counts_int = arrived_counts.astype(jnp.int32)
    placer = place_table(counts_int, payload.shape[2])
    merged = jnp.einsum(
        "jsxc,sxcd->xjd", placer, payload, preferred_element_type=jnp.float32
    ).astype(jnp.bfloat16)
    local_totals = jnp.sum(counts_int, axis=0)
    return (merged, local_totals)


def shards(tokens, expert_ids):
    owners = lax.axis_size("ep")
    row_count = tokens.shape[0]
    local_experts = EXPERTS // owners
    capacity = CAP
    labels = jnp.arange(EXPERTS, dtype=jnp.int32)
    route_hits = jnp.sum(
        (expert_ids[:, :, None] == labels[None, None, :]).astype(jnp.int32), axis=1
    )
    earlier = jnp.cumsum(route_hits, axis=0) - route_hits
    counts = jnp.sum(route_hits, axis=0)
    slot_index = jnp.arange(capacity, dtype=jnp.int32)
    placer = (route_hits.T[:, None, :] == 1) & (earlier.T[:, None, :] == slot_index[None, :, None])
    placer = placer.astype(jnp.bfloat16).reshape(EXPERTS * capacity, row_count)
    payload = jnp.dot(placer, tokens, preferred_element_type=jnp.float32).astype(jnp.bfloat16)
    payload = payload.reshape(owners, local_experts, capacity, tokens.shape[1])
    count_send = counts.reshape(owners, local_experts).astype(jnp.bfloat16)
    arrived, arrived_counts = side_by_side((payload, count_send), "ep", 0, 0, 2)
    merged, local_totals = compact((arrived, arrived_counts))
    return (merged, local_totals)


def solution(mesh):
    in_specs = (P("ep", None), P("ep", None))
    out_specs = (P("ep", None, None), P("ep"))
    return jax.shard_map(shards, mesh=mesh, in_specs=in_specs, out_specs=out_specs, check_vma=False)
```

profile of v0, /device:TPU:1, one launch (start us, length us, event | category | flops | bytes accessed | tf_op | source)
XLA Modules:
  0.0 443.7 jit_solution(16893146702671837955)
XLA Ops:
  0.6 0.9 copy.17
  1.6 0.4 convert_reduce_fusion.1
  2.0 0.1 copy.18
  2.2 0.2 convert_element_type.37
  2.4 0.2 reduce_window_sum.22
  2.6 0.1 copy.19
  2.7 0.1 eq.65
  2.9 0.1 and.19
  3.0 0.2 and.20
  3.2 0.1 eq.62
  3.2 1.0 eq.63
  4.2 12.1 %convolution_convert_fusion = bf16[1536,7168]{1,0:T(8,128)(2,1)} fusion(bf16[128,7168]{1,0:T(8,128)(2,1)S(1)} %copy-done, pred[1536,128]{1,0:T(32,128)(4,1)S(1)} %and.20, s32[1536,128]{1,0:T(8,128)} %eq.63, s32[1536]{0:T(1024)S(1)} %eq.65), kind=kOutput, calls=%fused_computation.1 | convolution fusion | flops 2829975552 | bytes 24844288 | tf_op jit(solution)/shard_map/dot_general | solution.py:61
  16.3 30.6 %reshape_reshape.3 = bf16[128,2,43008]{2,1,0:T(2,128)(2,1)} reshape(bf16[1536,7168]{1,0:T(8,128)(2,1)} %convolution_convert_fusion) | data formatting | bytes 44040192 | tf_op jit(solution)/shard_map/reshape;reshape | solution.py:11
  46.8 31.0 %pad_maximum_fusion = bf16[128,2,43009]{2,1,0:T(2,128)(2,1)S(1)} fusion(bf16[128,2,1]{2,1,0:T(2,128)(2,1)S(1)} %convert_element_type.37, bf16[128,2,43008]{2,1,0:T(2,128)(2,1)} %reshape_reshape.3), kind=kLoop, calls=%fused_computation.2 | loop fusion | flops 44041216 | bytes 44041216 | tf_op jit(solution)/shard_map/concatenate | solution.py:12
  77.8 255.9 %all_to_all.5 = bf16[128,2,43009]{2,1,0:T(2,128)(2,1)S(1)} all-to-all(bf16[128,2,43009]{2,1,0:T(2,128)(2,1)S(1)} %pad_maximum_fusion), channel_id=1, replica_groups=mesh['ep'=128] {'ep'}, dimensions={0} | all-to-all | bytes 44041216 | tf_op jit(solution)/shard_map/all_to_all | solution.py:14
  333.7 7.3 %copy-done.2 = bf16[128,2,43009]{2,1,0:T(2,128)(2,1)} copy-done((bf16[128,2,43009]{2,1,0:T(2,128)(2,1)}, bf16[128,2,43009]{2,1,0:T(2,128)(2,1)S(1)}, u32[]{:S(2)}) %copy-start.2) | copy-done | bytes 22020632
  341.1 0.1 convert_subtract_fusion
  341.2 0.1 copy.22
  341.3 0.9 slice_convert_fusion
  342.2 0.1 copy.21
  342.3 18.2 %slice.9 = bf16[128,2,43008]{2,1,0:T(2,128)(2,1)} slice(bf16[128,2,43009]{2,1,0:T(2,128)(2,1)} %copy-done.2), slice={[0:128], [0:2], [0:43008]} | slice | bytes 44040192 | tf_op jit(solution)/shard_map/slice | solution.py:19
  360.5 53.4 %copy.23 = bf16[128,2,43008]{0,2,1:T(8,128)(2,1)} copy(bf16[128,2,43008]{2,1,0:T(2,128)(2,1)} %slice.9) | data formatting | bytes 44040192 | tf_op jit(solution)/shard_map/slice | solution.py:19
  413.9 28.2 %bitcast_convert_fusion = bf16[2,768,7168]{2,1,0:T(8,128)(2,1)} fusion(bf16[128,2,6,7168]{0,3,2,1:T(8,128)(2,1)} %bitcast.12, s32[128,2,6]{0,2,1:T(8,128)S(1)} %iota_add_fusion, pred[128,2,6]{0,2,1:T(8,128)(4,1)S(1)} %iota_compare_fusion.2), kind=kOutput, calls=%fused_computation | convolution fusion | flops 16924803072 | bytes 44047872 | tf_op jit(solution)/shard_map/jsxc,sxcd->xjd/dot_general | solution.py:40
  442.1 1.6 convert_reduce_fusion.2
  (11 shorter events, 0.1 us)
Async XLA Ops:
  0.6 3.6 copy-start
  333.7 7.3 %copy-start.2 = (bf16[128,2,43009]{2,1,0:T(2,128)(2,1)}, bf16[128,2,43009]{2,1,0:T(2,128)(2,1)S(1)}, u32[]{:S(2)}) copy-start(bf16[128,2,43009]{2,1,0:T(2,128)(2,1)S(1)} %all_to_all.5) | copy-start | bytes 66061828
  413.9 29.8 %copy-start.1 = (bf16[128,7168]{1,0:T(8,128)(2,1)S(1)}, bf16[128,7168]{1,0:T(8,128)(2,1)}, u32[]{:S(2)}) copy-start(bf16[128,7168]{1,0:T(8,128)(2,1)} %param.2) | copy-start | bytes 5505028
where the time goes:
time: 451 us; the launch traced here: 444 us
  blocking collectives  256 us (57%)
  local copies, waits for them, and re-layouts  112 us (25%)
  matrix products  40.3 us (9%)
  other arithmetic  34.3 us (8%)
    all_to_all x1, blocking collectives, side_by_side(): lax.all_to_all(both, axis, split_axis=split_dim, concat_axis=concat_dim,...  256 us
    slice x2, local copies, waits for them, and re-layouts, side_by_side(): piece = result[..., at:at + column.shape[along]]  71.6 us
    concatenate x1, other arithmetic, side_by_side(): both = jnp.concatenate(columns, axis=along)  31 us
    another operation x1, local copies, waits for them, and re-layouts, side_by_side(): columns = [a.reshape(*a.shape[:along], -1) for a in arrays]  30.6 us
    dot_general x1, matrix products, compact(): jnp.einsum('jsxc,sxcd->xjd', placer, payload, preferred_element_type=jnp....  28.2 us
    dot_general x1, matrix products, shards(): jnp.dot(placer, tokens, preferred_element_type=jnp.float32)  12.1 us

commit v1 on v0

v1 whole, which is shorter than its diff:
```python
import functools

import jax
import jax.numpy as jnp
from jax import lax
from jax.experimental import pallas as pl
from jax.experimental.pallas import tpu as pltpu
from jax.sharding import PartitionSpec as P

EXPERTS = 256
CAP = 6
TOP = 8
TOK = 128
WIDTH = 7168
HALF = WIDTH // 2
QUARTER = HALF // 2
PIECE = QUARTER // 2
LINES = 768
SPLITS = ((0, 640), (640, 640), (1280, 512))
MESH = pl.DeviceIdType.MESH


def near(v):
    return v + 1 - 2 * (v % 2)


def far(v):
    return 3 - v


SHARE = (near, far)
CROSS = (far, near)
PAIR = (lambda v: v // 2, lambda v: ((v + 1) // 2) % 2)
MEMBER = (lambda v: v % 2, lambda v: v // 2)
ORDER = (None, (0, 3, 1, 2))


def pick(flag, flipped, value):
    return value + flag * (flipped - value)


def exchange(tok, ids, out, xg, oh, sb, mk, rk, load_sem, swap_send, swap_recv,
             ag_send, ag_recv, put_send, put_recv, keep_sem):
    me = lax.axis_index("ep")
    core, x, z, y = me % 2, (me // 2) % 4, (me // 8) % 4, me // 32

    def device(yy, zz, xx, cc):
        return ((yy * 4 + zz) * 4 + xx) * 2 + cc

    def target(h, d):
        flip = CROSS[h]
        return device(
            pick(d // 8, flip(y), y),
            pick((d // 4) % 2, flip(z), z),
            pick((d // 2) % 2, flip(x), x),
            pick(d % 2, 1 - core, core),
        )

    loads = []
    for h in range(2):
        copy = pltpu.make_async_copy(
            tok.at[:, pl.ds(pl.multiple_of(h * HALF + core * QUARTER, 128), QUARTER)],
            xg.at[h, 0, pl.ds(pl.multiple_of(core * TOK, TOK), TOK), :],
            load_sem.at[h],
        )
        copy.start()
        loads.append(copy)

    barrier = pltpu.get_barrier_semaphore()
    for h in range(2):
        for d in range(1, 16):
            if h == 0 or d >= 2:
                pl.semaphore_signal(barrier, inc=1, device_id=(target(h, d),), device_id_type=MESH)
    pl.semaphore_wait(barrier, 29)

    partner = device(y, z, x, 1 - core)
    swaps = []
    for h in range(2):
        copy = pltpu.make_async_remote_copy(
            src_ref=tok.at[:, pl.ds(pl.multiple_of(h * HALF + (1 - core) * QUARTER, 128), QUARTER)],
            dst_ref=xg.at[h, 0, pl.ds(pl.multiple_of(core * TOK, TOK), TOK), :],
            send_sem=swap_send.at[h],
            recv_sem=swap_recv.at[h],
            device_id=(partner,),
            device_id_type=MESH,
        )
        copy.start()
        swaps.append(copy)

    def neighbour(h, bit):
        flip = SHARE[h]
        if bit == 1:
            return device(y, z, flip(x), core)
        if bit == 2:
            return device(y, flip(z), x, core)
        return device(flip(y), z, x, core)

    def spread(h, i, slot, bit):
        at, size = SPLITS[i]
        return pltpu.make_async_remote_copy(
            src_ref=xg.at[h, slot, :, pl.ds(at, size)],
            dst_ref=xg.at[h, slot ^ bit, :, pl.ds(at, size)],
            send_sem=ag_send.at[h, i, slot ^ bit],
            recv_sem=ag_recv.at[h, i, slot ^ bit],
            device_id=(neighbour(h, bit),),
            device_id_type=MESH,
        )

    def step_slots(i, step):
        bits = [(1, 2, 4)[(i + k) % 3] for k in range(3)]
        held = [0]
        for k in range(step):
            held += [s ^ bits[k] for s in held]
        return held, bits[step]

    def all_spread(step):
        copies = []
        for i in range(3):
            held, bit = step_slots(i, step)
            for slot in held:
                for h in range(2):
                    copies.append(spread(h, i, slot, bit))
        return copies

    sub = lax.broadcasted_iota(jnp.int32, (16, TOK), 0) % 8
    before = lax.broadcasted_iota(jnp.int32, (TOK, TOK), 0)
    after = lax.broadcasted_iota(jnp.int32, (TOK, TOK), 1)
    earlier = jnp.where(before < after, 1.0, 0.0).astype(jnp.bfloat16)

    def group_row(h, g):
        return pick(g, SHARE[h](y), y), PAIR[h](z) * 2 + PAIR[h](x)

    def build(h, g):
        ys, block = group_row(h, g)
        names = [ids[h, ys * 4 + block, k] for k in range(8)]

        def marks(d, carry):
            owner = target(h, d)
            for e in range(2):
                hit = names[0] == owner * 2 + e
                for k in range(1, 8):
                    hit = hit | (names[k] == owner * 2 + e)
                mk[pl.ds(pl.multiple_of(d * 16 + e * 8, 8), 8), :] = jnp.where(hit, 1.0, 0.0)
            return carry

        lax.fori_loop(0, 16, marks, 0)
        marked = mk[...]
        rank = jnp.dot(marked.astype(jnp.bfloat16), earlier, preferred_element_type=jnp.float32)
        rk[...] = jnp.where(marked > 0.5, rank, -1.0)

        def places(d, carry):
            for e in range(2):
                rank_e = rk[pl.ds(pl.multiple_of(d * 16 + e * 8, 8), 8), :]
                for j in range(0, CAP, 2):
                    hit = jnp.concatenate(
                        [jnp.where(rank_e == float(j + q), 1.0, 0.0) for q in range(2)], axis=0
                    )
                    for k in range(8):
                        own = (
                            pick(k // 4, 1 - MEMBER[h](z), MEMBER[h](z)) * 4
                            + pick((k // 2) % 2, 1 - MEMBER[h](x), MEMBER[h](x)) * 2
                            + k % 2
                        )
                        oh[h, g, d, e * 48 + j * 8 : e * 48 + j * 8 + 16, k * TOK : (k + 1) * TOK] = (
                            jnp.where(sub == own, hit, 0.0).astype(jnp.bfloat16)
                        )
            return carry

        lax.fori_loop(0, 16, places, 0)

    for copy in loads:
        copy.wait()
    for copy in swaps:
        copy.wait_recv()
    first = all_spread(0)
    for copy in first:
        copy.start()
    build(0, 0)
    for copy in first:
        copy.wait_recv()
    second = all_spread(1)
    for copy in second:
        copy.start()
    build(1, 0)
    for copy in second:
        copy.wait_recv()
    third = all_spread(2)
    for copy in third:
        copy.start()
    build(0, 1)
    build(1, 1)
    for copy in third:
        copy.wait_recv()

    def put(h, u, d):
        g, n = u // 8, (u // 4) % 2
        ys, block = group_row(h, g)
        return (
            sb.at[h, u // 4, d],
            out.at[
                h,
                :,
                pl.ds(pl.multiple_of(ys * 192 + block * 48, 16), 48),
                pl.ds(pl.multiple_of(core * QUARTER + n * PIECE, 128), PIECE),
            ],
        )

    def remote(h, u, d):
        src, dst = put(h, u, d)
        return pltpu.make_async_remote_copy(
            src_ref=src,
            dst_ref=dst,
            send_sem=put_send.at[h, u // 4, d],
            recv_sem=put_recv.at[h, u // 4, d],
            device_id=(target(h, d),),
            device_id_type=MESH,
        )

    def local(h, u):
        src, dst = put(h, u, 0)
        return pltpu.make_async_copy(src, dst, keep_sem.at[h, u // 4])

    def send(h, u):
        for q in range(4):
            d = (u % 4) * 4 + q
            if q == 0:
                @pl.when(u % 4 == 0)
                def _():
                    local(h, u).start()

                @pl.when(u % 4 != 0)
                def _():
                    remote(h, u, d).start()
            else:
                remote(h, u, d).start()

    def pack(u, carry):
        g, n, m = u // 8, (u // 4) % 2, u % 4
        for h in range(2):
            placer = oh[h, g, pl.ds(m * 4, 4)].reshape(384, 1024)
            rows = xg[h, pl.ds(g * 4, 4), :, pl.ds(pl.multiple_of(n * PIECE, 128), PIECE)]
            packed = jnp.dot(placer, rows.reshape(1024, PIECE), preferred_element_type=jnp.float32)
            sb[h, u // 4, pl.ds(m * 4, 4)] = packed.astype(jnp.bfloat16).reshape(4, 2, 48, PIECE)

            @pl.when(u > 0)
            def _():
                send(h, u - 1)
        return carry

    lax.fori_loop(0, 16, pack, 0)
    for h in range(2):
        send(h, 15)

    for copy in first + second + third:
        copy.wait_send()
    for copy in swaps:
        copy.wait_send()

    def drain(w, carry):
        for h in range(2):
            local(h, w * 4).wait()

            def one(d, inner):
                remote(h, w * 4, d).wait()
                return inner

            lax.fori_loop(1, 16, one, 0)
        return carry

    lax.fori_loop(0, 4, drain, 0)


def place(goal, rows, out, placer):
    @pl.when(pl.program_id(2) == 0)
    def _():
        line = lax.broadcasted_iota(jnp.int32, (LINES, LINES), 0)
        placer[...] = jnp.where(goal[0, 0] == line, 1.0, 0.0).astype(jnp.bfloat16)

    out[0] = jnp.dot(placer[...], rows[0, 0], preferred_element_type=jnp.float32).astype(jnp.bfloat16)


def regroup(table, h):
    if ORDER[h] is not None:
        table = jnp.concatenate([table[:, i : i + 1] for i in ORDER[h]], axis=1)
        table = jnp.concatenate([table[:, :, i : i + 1] for i in ORDER[h]], axis=2)
    rest = table.shape[4:]
    table = table.reshape(4, 2, 2, 2, 2, 2, *rest)
    return jnp.transpose(table, (0, 1, 3, 2, 4, 5) + tuple(range(6, 6 + len(rest))))


def shards(tokens, expert_ids):
    me = lax.axis_index("ep")
    every = lax.all_gather(expert_ids.T, "ep")
    grid = every.reshape(4, 4, 4, 2, TOP, TOK)
    ids = jnp.stack(
        [
            jnp.transpose(regroup(grid, h).reshape(16, 8, TOP, TOK), (0, 2, 1, 3))
            for h in range(2)
        ]
    )
    mine = me * 2 + jnp.arange(2, dtype=jnp.int32)
    counts = jnp.sum((every[:, :, :, None] == mine).astype(jnp.int32), axis=(1, 2))
    index = jnp.arange(128, dtype=jnp.int32)
    offsets = jnp.sum(
        jnp.where(index[:, None, None] > index[None, :, None], counts[None], 0), axis=1
    )
    totals = jnp.sum(counts, axis=0)
    slot = jnp.arange(CAP, dtype=jnp.int32)[:, None]
    goals = []
    for h in range(2):
        have = regroup(counts.reshape(4, 4, 4, 2, 2), h).reshape(16, 1, 8, 2)
        start = regroup(offsets.reshape(4, 4, 4, 2, 2), h).reshape(16, 1, 8, 2)
        goal = jnp.where(slot[None, :, :, None] < have, start + slot[None, :, :, None], -1)
        goals.append(jnp.transpose(goal.reshape(LINES, 2)))
    goals = jnp.stack(goals).reshape(2, 2, 1, LINES)

    arrived = pl.pallas_call(
        exchange,
        out_shape=jax.ShapeDtypeStruct((2, 2, LINES, HALF), jnp.bfloat16),
        in_specs=[
            pl.BlockSpec(memory_space=pl.ANY),
            pl.BlockSpec(memory_space=pltpu.VMEM),
        ],
        out_specs=pl.BlockSpec(memory_space=pl.ANY),
        scratch_shapes=[
            pltpu.VMEM((2, 8, 2 * TOK, QUARTER), jnp.bfloat16),
            pltpu.VMEM((2, 2, 16, 96, 8 * TOK), jnp.bfloat16),
            pltpu.VMEM((2, 4, 16, 2, 48, PIECE), jnp.bfloat16),
            pltpu.VMEM((256, TOK), jnp.float32),
            pltpu.VMEM((256, TOK), jnp.float32),
            pltpu.SemaphoreType.DMA((2,)),
            pltpu.SemaphoreType.DMA((2,)),
            pltpu.SemaphoreType.DMA((2,)),
            pltpu.SemaphoreType.DMA((2, 3, 8)),
            pltpu.SemaphoreType.DMA((2, 3, 8)),
            pltpu.SemaphoreType.DMA((2, 4, 16)),
            pltpu.SemaphoreType.DMA((2, 4, 16)),
            pltpu.SemaphoreType.DMA((2, 4)),
        ],
        compiler_params=pltpu.CompilerParams(
            collective_id=0, has_side_effects=True, vmem_limit_bytes=62 * 1024 * 1024
        ),
        name="exchange",
    )(tokens, ids)

    merged = pl.pallas_call(
        place,
        out_shape=jax.ShapeDtypeStruct((2, LINES, WIDTH), jnp.bfloat16),
        grid=(2, 2, 4),
        in_specs=[
            pl.BlockSpec((1, 1, 1, LINES), lambda e, h, n: (h, e, 0, 0)),
            pl.BlockSpec((1, 1, LINES, HALF // 4), lambda e, h, n: (h, e, 0, n)),
        ],
        out_specs=pl.BlockSpec((1, LINES, HALF // 4), lambda e, h, n: (e, 0, h * 4 + n)),
        scratch_shapes=[pltpu.VMEM((LINES, LINES), jnp.bfloat16)],
        name="place",
    )(goals, arrived)
    return (merged, totals)


def solution(mesh):
    in_specs = (P("ep", None), P("ep", None))
    out_specs = (P("ep", None, None), P("ep"))
    return jax.shard_map(shards, mesh=mesh, in_specs=in_specs, out_specs=out_specs, check_vma=False)
```

time: 451 us -> 279 us (0.62)
  Pallas kernels: 0 us -> 224 us
  blocking collectives: 256 us -> 39.5 us
  local copies, waits for them, and re-layouts: 112 us -> 4.27 us
  matrix products: 40.3 us -> 0 us
  other arithmetic: 34.3 us -> 6.25 us
    all_to_all x1 -> x0, blocking collectives: 256 us -> none  [side_by_side(): lax.all_to_all(both, axis, split_axis=split_dim, concat_axis=concat_dim,...]
    pallas_call x0 -> x2, Pallas kernels: none -> 224 us  [the longest x1 195 us: shards(): pl.pallas_call(exchange, out_shape=jax.ShapeDtypeStruct((2, 2, LINES, HAL...]
    slice x2 -> x6, local copies, waits for them, and re-layouts: 71.6 us -> 0.06 us  [regroup(): table = jnp.concatenate([table[:, i:i + 1] for i in ORDER[h]], axis=1)]
    dot_general x2 -> x0, matrix products: 40.3 us -> none  [the longest x1 28.2 us: compact(): jnp.einsum('jsxc,sxcd->xjd', placer, payload, preferred_element_type=jnp....]
    all_gather x0 -> x1, blocking collectives: none -> 39.5 us  [shards(): every = lax.all_gather(expert_ids.T, 'ep')]
    concatenate x1 -> x6, other arithmetic: 31 us -> 0.22 us  [the longest x3 0.15 us: regroup(): table = jnp.concatenate([table[:, :, i:i + 1] for i in ORDER[h]], axis=2)]
    another operation x1 -> x3, local copies, waits for them, and re-layouts: 30.6 us -> 0.61 us  [regroup(): table = table.reshape(4, 2, 2, 2, 2, 2, *rest)]
    unnamed x7 -> x0, local copies, waits for them, and re-layouts: 8.26 us -> none
where the time goes in v1:
time: 279 us; the launch traced here: 275 us
  Pallas kernels  224 us (80%)
  blocking collectives  39.5 us (14%)
  other arithmetic  6.25 us (2%)
  local copies, waits for them, and re-layouts  4.27 us (2%)
    pallas_call x1, Pallas kernels, shards(): pl.pallas_call(exchange, out_shape=jax.ShapeDtypeStruct((2, 2, LINES, HAL...  195 us
    all_gather x1, blocking collectives, shards(): every = lax.all_gather(expert_ids.T, 'ep')  39.5 us
    pallas_call x1, Pallas kernels, shards(): pl.pallas_call(place, out_shape=jax.ShapeDtypeStruct((2, LINES, WIDTH), j...  28.9 us

profile of v1, /device:TPU:1, one launch (start us, length us, event | category | flops | bytes accessed | tf_op | source)
XLA Modules:
  0.0 275.3 jit_solution(14326113768531980805)
XLA Ops:
  0.8 39.5 %all-gather = s32[1024,128]{1,0:T(8,128)S(1)} all-gather(s32[8,128]{1,0:T(8,128)} %bitcast.70), channel_id=2, replica_groups=mesh['ep'=128] {'ep'}, dimensions={0}, use_global_device_ids=true | all-gather | bytes 528384 | tf_op jit(solution)/shard_map/all_gather | solution.py:293
  40.3 4.7 %convert_reduce_fusion = (s32[2]{0:T(128)}, s32[128,2]{1,0:T(8,128)S(1)}) fusion(s32[128,8,128]{2,1,0:T(8,128)S(1)} %bitcast.59, s32[2]{0:T(128)S(1)} %iota_add_fusion), kind=kLoop, calls=%fused_computation | loop fusion | flops 1048318 | bytes 525328 | tf_op jit(solution)/shard_map/reduce_sum | solution.py:307
  45.0 0.1 select_reduce_fusion
  45.2 0.2 reshape.72
  45.5 0.3 copy.39
  45.8 0.3 copy.47
  46.1 0.1 reshape.85
  46.3 0.2 reshape_reshape.10
  46.5 0.1 reshape.83
  46.6 0.2 reshape.70
  46.9 0.3 copy.36
  47.2 0.3 copy.46
  47.5 0.1 reshape.84
  47.6 0.2 reshape_reshape.9
  47.8 0.1 reshape.82
  48.0 0.1 lt.61
  48.1 0.1 lt.65
  48.2 0.1 add.46
  48.5 0.6 reshape.74.goal
  49.3 0.3 copy.43
  49.5 0.3 copy.42
  49.8 1.1 pad_add_fusion.ids
  50.9 195.4 %exchange.1.rows = bf16[2,2,768,3584]{3,2,1,0:T(8,128)(2,1)} custom-call(bf16[128,7168]{1,0:T(8,128)(2,1)} %tok.1, s32[2,16,8,8,128]{4,3,2,1,0:T(8,128)} %pad_add_fusion.ids), custom_call_target="tpu_custom_call" | custom-call | tf_op jit(solution)/shard_map/exchange/pallas_call | solution.py:317
  246.4 28.9 %place.1 = bf16[2,768,7168]{2,1,0:T(8,128)(2,1)} custom-call(s32[2,2,1,768]{3,2,1,0:T(1,128)} %reshape.74.goal, bf16[2,2,768,3584]{3,2,1,0:T(8,128)(2,1)} %exchange.1.rows), custom_call_target="tpu_custom_call" | custom-call | tf_op jit(solution)/shard_map/place/pallas_call | solution.py:346
  (29 shorter events, 0.7 us)

commit v2 on v1

v2 whole, which is shorter than its diff:
```python
import functools

import jax
import jax.numpy as jnp
from jax import lax
from jax.experimental import pallas as pl
from jax.experimental.pallas import tpu as pltpu
from jax.sharding import PartitionSpec as P

EXPERTS = 256
CAP = 6
TOP = 8
TOK = 128
WIDTH = 7168
HALF = WIDTH // 2
QUARTER = HALF // 2
PIECE = QUARTER // 2
LINES = 768
SPLITS = (((0, 384), (384, 256), (640, 256)), ((896, 256), (1152, 384), (1536, 256)))
MESH = pl.DeviceIdType.MESH
WINDOW = 208


def near(v):
    return v + 1 - 2 * (v % 2)


def far(v):
    return 3 - v


SHARE = (near, far)
CROSS = (far, near)
PAIR = (lambda v: v // 2, lambda v: ((v + 1) // 2) % 2)
MEMBER = (lambda v: v % 2, lambda v: v // 2)
SPOT = (lambda p, m: p * 2 + m, lambda p, m: p + m * (3 - 2 * p))


def pick(flag, flipped, value):
    return value + flag * (flipped - value)


def exchange(tok, ids, out, goal, starts, xg, oh, sb, mk, rk, idr, cts, ctr,
             load_sem, swap_send, swap_recv, id_sem, id_send, id_recv, ag_send, ag_recv,
             count_send, count_recv, put_send, put_recv, keep_sem):
    me = lax.axis_index("ep")
    core, x, z, y = me % 2, (me // 2) % 4, (me // 8) % 4, me // 32

    def device(yy, zz, xx, cc):
        return ((yy * 4 + zz) * 4 + xx) * 2 + cc

    def target(flip, d):
        return device(
            pick(d // 8, flip(y), y),
            pick((d // 4) % 2, flip(z), z),
            pick((d // 2) % 2, flip(x), x),
            pick(d % 2, 1 - core, core),
        )

    loads = []
    for h in range(2):
        loads.append(
            pltpu.make_async_copy(
                tok.at[:, pl.ds(pl.multiple_of(h * HALF + core * QUARTER, 128), QUARTER)],
                xg.at[h, 0, pl.ds(pl.multiple_of(core * TOK, TOK), TOK), :],
                load_sem.at[h],
            )
        )
        loads.append(pltpu.make_async_copy(ids, idr.at[h, 0], id_sem.at[h]))
    for copy in loads:
        copy.start()

    barrier = pltpu.get_barrier_semaphore()
    for h in range(2):
        for d in range(1, 16):
            if h == 0 or d >= 2:
                pl.semaphore_signal(
                    barrier, inc=1, device_id=(target(CROSS[h], d),), device_id_type=MESH
                )
    pl.semaphore_wait(barrier, 29)

    partner = device(y, z, x, 1 - core)
    swaps = []
    for h in range(2):
        copy = pltpu.make_async_remote_copy(
            src_ref=tok.at[:, pl.ds(pl.multiple_of(h * HALF + (1 - core) * QUARTER, 128), QUARTER)],
            dst_ref=xg.at[h, 0, pl.ds(pl.multiple_of(core * TOK, TOK), TOK), :],
            send_sem=swap_send.at[h],
            recv_sem=swap_recv.at[h],
            device_id=(partner,),
            device_id_type=MESH,
        )
        copy.start()
        swaps.append(copy)
    names_sent = []
    for d in range(1, 16):
        for h in range(2):
            copy = pltpu.make_async_remote_copy(
                src_ref=ids,
                dst_ref=idr.at[h, d],
                send_sem=id_send.at[h, d],
                recv_sem=id_recv.at[h, d],
                device_id=(target(SHARE[h], d),),
                device_id_type=MESH,
            )
            copy.start()
            names_sent.append(copy)

    def neighbour(h, bit):
        flip = SHARE[h]
        if bit == 1:
            return device(y, z, flip(x), core)
        if bit == 2:
            return device(y, flip(z), x, core)
        return device(flip(y), z, x, core)

    def spread(h, n, i, slot, bit):
        at, size = SPLITS[n][i]
        return pltpu.make_async_remote_copy(
            src_ref=xg.at[h, slot, :, pl.ds(at, size)],
            dst_ref=xg.at[h, slot ^ bit, :, pl.ds(at, size)],
            send_sem=ag_send.at[h, n, i, slot ^ bit],
            recv_sem=ag_recv.at[h, n, i, slot ^ bit],
            device_id=(neighbour(h, bit),),
            device_id_type=MESH,
        )

    def spread_step(n, step):
        copies = []
        for i in range(3):
            bits = [(1, 2, 4)[(i + k) % 3] for k in range(3)]
            held = [0]
            for k in range(step):
                held += [s ^ bits[k] for s in held]
            for slot in held:
                for h in range(2):
                    copies.append(spread(h, n, i, slot, bits[step]))
        return copies

    sub = lax.broadcasted_iota(jnp.int32, (16, TOK), 0) % 8
    lane = lax.broadcasted_iota(jnp.int32, (8, TOK), 1)
    before = lax.broadcasted_iota(jnp.int32, (TOK, TOK), 0)
    after = lax.broadcasted_iota(jnp.int32, (TOK, TOK), 1)
    earlier = jnp.where(before < after, 1.0, 0.0).astype(jnp.bfloat16)
    ones = jnp.ones((TOK, TOK), jnp.bfloat16)

    def group_row(h, g):
        return pick(g, SHARE[h](y), y), PAIR[h](z) * 2 + PAIR[h](x)

    def source_place(h, k):
        return (
            pick(k // 4, 1 - MEMBER[h](z), MEMBER[h](z)) * 4
            + pick((k // 2) % 2, 1 - MEMBER[h](x), MEMBER[h](x)) * 2
            + k % 2
        )

    def build(h, g):
        slots = [(g * 4 + k // 2) * 2 + pick(k % 2, 1 - core, core) for k in range(8)]
        names = []
        for q in range(TOP):
            rows = jnp.zeros((8, TOK), jnp.int32)
            for k in range(8):
                rows = jnp.where(sub[:8] == source_place(h, k), idr[h, slots[k], q : q + 1, :], rows)
            names.append(rows)

        def marks(d, carry):
            owner = target(CROSS[h], d)
            for e in range(2):
                hit = names[0] == owner * 2 + e
                for q in range(1, TOP):
                    hit = hit | (names[q] == owner * 2 + e)
                mk[pl.ds(pl.multiple_of(d * 16 + e * 8, 8), 8), :] = jnp.where(hit, 1.0, 0.0)
            return carry

        lax.fori_loop(0, 16, marks, 0)
        marked = mk[...]
        whole = marked.astype(jnp.bfloat16)
        rank = jnp.dot(whole, earlier, preferred_element_type=jnp.float32)
        rk[...] = jnp.where(marked > 0.5, rank, -1.0)
        if h == 0:
            mk[...] = jnp.dot(whole, ones, preferred_element_type=jnp.float32)
            member = pick(g, 1 - y % 2, y % 2)
            for flips in range(8):
                tile = cts[flips]
                for e in range(2):
                    tile = jnp.where(
                        lane // 32 == member * 2 + e,
                        mk[flips * 32 + e * 8 : flips * 32 + e * 8 + 8, :],
                        tile,
                    )
                cts[flips] = tile

        def places(d, carry):
            for e in range(2):
                rank_e = rk[pl.ds(pl.multiple_of(d * 16 + e * 8, 8), 8), :]
                for j in range(0, CAP, 2):
                    hit = jnp.concatenate(
                        [jnp.where(rank_e == float(j + q), 1.0, 0.0) for q in range(2)], axis=0
                    )
                    for k in range(8):
                        oh[h, g, d, e * 48 + j * 8 : e * 48 + j * 8 + 16, k * TOK : (k + 1) * TOK] = (
                            jnp.where(sub == source_place(h, k), hit, 0.0).astype(jnp.bfloat16)
                        )
            return carry

        lax.fori_loop(0, 16, places, 0)

    cts[...] = jnp.zeros(cts.shape, jnp.float32)
    for copy in loads:
        copy.wait()
    for copy in swaps:
        copy.wait_recv()
    first = [spread_step(n, 0) for n in range(2)]
    for n in range(2):
        for copy in first[n]:
            copy.start()
    for copy in names_sent:
        copy.wait_recv()
    build(0, 0)
    second = [spread_step(n, 1) for n in range(2)]
    for n in range(2):
        for copy in first[n]:
            copy.wait_recv()
        for copy in second[n]:
            copy.start()
    build(0, 1)
    third = [spread_step(n, 2) for n in range(2)]
    for n in range(2):
        for copy in second[n]:
            copy.wait_recv()
        for copy in third[n]:
            copy.start()

    block = (y // 2) * 4 + (z // 2) * 2 + x // 2
    counts = []
    for flips in range(1, 8):
        copy = pltpu.make_async_remote_copy(
            src_ref=cts.at[flips],
            dst_ref=ctr.at[block],
            send_sem=count_send.at[flips],
            recv_sem=count_recv.at[flips],
            device_id=(target(far, flips * 2),),
            device_id_type=MESH,
        )
        copy.start()
        counts.append(copy)
    own_count = pltpu.make_async_copy(cts.at[0], ctr.at[block], count_send.at[0])
    own_count.start()
    build(1, 0)
    build(1, 1)

    def put(h, n, w, d):
        ys, where = group_row(h, w // 4)
        return (
            sb.at[h, n, w // 4, d],
            out.at[
                h,
                :,
                pl.ds(pl.multiple_of(ys * 192 + where * 48, 16), 48),
                pl.ds(pl.multiple_of(core * QUARTER + n * PIECE, 128), PIECE),
            ],
        )

    def remote(h, n, w, d):
        src, dst = put(h, n, w, d)
        return pltpu.make_async_remote_copy(
            src_ref=src,
            dst_ref=dst,
            send_sem=put_send.at[h, n, w // 4, d],
            recv_sem=put_recv.at[h, n, w // 4, d],
            device_id=(target(CROSS[h], d),),
            device_id_type=MESH,
        )

    def local(h, n, w):
        src, dst = put(h, n, w, 0)
        return pltpu.make_async_copy(src, dst, keep_sem.at[h, n, w // 4])

    def send(h, n, w):
        for q in range(3, -1, -1):
            d = (3 - w % 4) * 4 + q
            if q == 0:
                @pl.when(w % 4 == 3)
                def _():
                    local(h, n, w).start()

                @pl.when(w % 4 != 3)
                def _():
                    remote(h, n, w, d).start()
            else:
                remote(h, n, w, d).start()

    for n in range(2):
        for copy in third[n]:
            copy.wait_recv()

        def pack(w, carry, n=n):
            g, m = w // 4, 3 - w % 4
            for h in range(2):
                placer = oh[h, g, pl.ds(m * 4, 4)].reshape(384, 1024)
                rows = xg[h, pl.ds(g * 4, 4), :, n * PIECE : (n + 1) * PIECE]
                packed = jnp.dot(
                    placer, rows.reshape(1024, PIECE), preferred_element_type=jnp.float32
                )
                sb[h, n, g, pl.ds(m * 4, 4)] = packed.astype(jnp.bfloat16).reshape(4, 2, 48, PIECE)

                @pl.when(w > 0)
                def _():
                    send(h, n, w - 1)
            return carry

        lax.fori_loop(0, 8, pack, 0)
        for h in range(2):
            send(h, n, 7)

    own_count.wait()
    for copy in counts:
        copy.wait_recv()
    table = ctr[...].reshape(64, TOK).astype(jnp.bfloat16)
    row = lax.broadcasted_iota(jnp.int32, (64, 192), 0)
    col = lax.broadcasted_iota(jnp.int32, (64, 192), 1)
    row_z = SPOT[0]((row // 16) % 2, (row // 4) % 2)
    row_x = SPOT[0]((row // 8) % 2, (row // 2) % 2)
    turn = (((0,), (0,)), ((), ()))
    slot = (lax.broadcasted_iota(jnp.int32, (1, 192), 1) % 48) // 8
    for h in range(2):
        col_z = SPOT[h](col // 96, (col % 8) // 4)
        col_x = SPOT[h]((col // 48) % 2, (col // 2) % 2)
        for yy in range(4):
            there = device(yy, col_z, col_x, col % 2)
            base = [jnp.zeros((1, 192), jnp.float32) for _ in range(2)]
            have = [jnp.zeros((1, 192), jnp.float32) for _ in range(2)]
            for member in range(2):
                here = device((row // 32) * 2 + member, row_z, row_x, row % 2)
                below = jnp.where(here < there, 1.0, 0.0).astype(jnp.bfloat16)
                same = jnp.where(here == there, 1.0, 0.0).astype(jnp.bfloat16)
                below = lax.dot_general(table, below, turn, preferred_element_type=jnp.float32)
                same = lax.dot_general(table, same, turn, preferred_element_type=jnp.float32)
                for e in range(2):
                    at = member * 64 + e * 32
                    base[e] = base[e] + below[at : at + 1, :]
                    have[e] = have[e] + same[at : at + 1, :]
            for e in range(2):
                at = base[e].astype(jnp.int32)
                mine = (h * 2 + e) * 4 + yy
                goal[mine : mine + 1, 0:192] = jnp.where(slot < have[e].astype(jnp.int32), at + slot, -1)
                if h == 0:
                    starts[e * 4 + yy : e * 4 + yy + 1, :] = at[:, 0:TOK]
    sums = lax.dot_general(
        table, jnp.ones((64, TOK), jnp.bfloat16), turn, preferred_element_type=jnp.float32
    )
    for e in range(2):
        starts[8 + e : 9 + e, :] = (
            sums[e * 32 : e * 32 + 1, :] + sums[64 + e * 32 : 65 + e * 32, :]
        ).astype(jnp.int32)

    for copy in names_sent + counts + swaps:
        copy.wait_send()
    for step in (first, second, third):
        for n in range(2):
            for copy in step[n]:
                copy.wait_send()

    for n in range(2):

        def drain(g, carry, n=n):
            for h in range(2):
                local(h, n, g * 4).wait()

                def one(d, inner, h=h):
                    remote(h, n, g * 4, d).wait()
                    return inner

                lax.fori_loop(1, 16, one, 0)
            return carry

        lax.fori_loop(0, 2, drain, 0)


def place(starts, goal, rows, out, totals, placer):
    e, h, n = pl.program_id(0), pl.program_id(1), pl.program_id(2)

    def window(yy):
        return pl.multiple_of(jnp.minimum(starts[e * 4 + yy, 0] // 16 * 16, LINES - WINDOW), 16)

    @pl.when(n == 0)
    def _():
        totals[e] = starts[8 + e, 0]
        line = lax.broadcasted_iota(jnp.int32, (WINDOW, 192), 0)
        for yy in range(4):
            wanted = goal[pl.ds((h * 2 + e) * 4 + yy, 1), 0:192] - window(yy)
            placer[yy] = jnp.where(wanted == line, 1.0, 0.0).astype(jnp.bfloat16)

    out[...] = jnp.zeros(out.shape, jnp.bfloat16)
    for yy in range(4):
        part = jnp.dot(
            placer[yy], rows[0, 0, yy * 192 : (yy + 1) * 192, :], preferred_element_type=jnp.float32
        ).astype(jnp.bfloat16)
        span = pl.ds(window(yy), WINDOW)
        out[0, span, :] = out[0, span, :] + part


def shards(tokens, expert_ids):
    anywhere = pl.BlockSpec(memory_space=pl.ANY)
    vmem = pl.BlockSpec(memory_space=pltpu.VMEM)
    arrived, goal, starts = pl.pallas_call(
        exchange,
        out_shape=(
            jax.ShapeDtypeStruct((2, 2, LINES, HALF), jnp.bfloat16),
            jax.ShapeDtypeStruct((16, 256), jnp.int32),
            jax.ShapeDtypeStruct((16, TOK), jnp.int32),
        ),
        in_specs=[anywhere, vmem],
        out_specs=(anywhere, vmem, vmem),
        scratch_shapes=[
            pltpu.VMEM((2, 8, 2 * TOK, QUARTER), jnp.bfloat16),
            pltpu.VMEM((2, 2, 16, 96, 8 * TOK), jnp.bfloat16),
            pltpu.VMEM((2, 2, 2, 16, 2, 48, PIECE), jnp.bfloat16),
            pltpu.VMEM((256, TOK), jnp.float32),
            pltpu.VMEM((256, TOK), jnp.float32),
            pltpu.VMEM((2, 16, TOP, TOK), jnp.int32),
            pltpu.VMEM((8, 8, TOK), jnp.float32),
            pltpu.VMEM((8, 8, TOK), jnp.float32),
            pltpu.SemaphoreType.DMA((2,)),
            pltpu.SemaphoreType.DMA((2,)),
            pltpu.SemaphoreType.DMA((2,)),
            pltpu.SemaphoreType.DMA((2,)),
            pltpu.SemaphoreType.DMA((2, 16)),
            pltpu.SemaphoreType.DMA((2, 16)),
            pltpu.SemaphoreType.DMA((2, 2, 3, 8)),
            pltpu.SemaphoreType.DMA((2, 2, 3, 8)),
            pltpu.SemaphoreType.DMA((8,)),
            pltpu.SemaphoreType.DMA((8,)),
            pltpu.SemaphoreType.DMA((2, 2, 2, 16)),
            pltpu.SemaphoreType.DMA((2, 2, 2, 16)),
            pltpu.SemaphoreType.DMA((2, 2, 2)),
        ],
        compiler_params=pltpu.CompilerParams(
            collective_id=0, has_side_effects=True, vmem_limit_bytes=62 * 1024 * 1024
        ),
        name="exchange",
    )(tokens, expert_ids.T)

    return pl.pallas_call(
        place,
        out_shape=(
            jax.ShapeDtypeStruct((2, LINES, WIDTH), jnp.bfloat16),
            jax.ShapeDtypeStruct((2,), jnp.int32),
        ),
        grid=(2, 2, 4),
        in_specs=[
            pl.BlockSpec(memory_space=pltpu.SMEM),
            vmem,
            pl.BlockSpec((1, 1, LINES, HALF // 4), lambda e, h, n: (h, e, 0, n)),
        ],
        out_specs=(
            pl.BlockSpec((1, LINES, HALF // 4), lambda e, h, n: (e, 0, h * 4 + n)),
            pl.BlockSpec(memory_space=pltpu.SMEM),
        ),
        scratch_shapes=[pltpu.VMEM((4, WINDOW, 192), jnp.bfloat16)],
        name="place",
    )(starts, goal, arrived)


def solution(mesh):
    in_specs = (P("ep", None), P("ep", None))
    out_specs = (P("ep", None, None), P("ep"))
    return jax.shard_map(shards, mesh=mesh, in_specs=in_specs, out_specs=out_specs, check_vma=False)
```

time: 279 us -> 231 us (0.83); the launches traced: 275 us -> 230 us
  blocking collectives: 39.5 us -> 0 us
  other arithmetic: 6.25 us -> 0 us
  Pallas kernels: 224 us -> 230 us
  local copies, waits for them, and re-layouts: 4.27 us -> 0 us
    all_gather x1 -> x0, blocking collectives: 39.5 us -> none  [shards(): every = lax.all_gather(expert_ids.T, 'ep')]
    pallas_call x2, Pallas kernels: 224 us -> 230 us  [the longest x1 205 us: shards(): pl.pallas_call(exchange, out_shape=(jax.ShapeDtypeStruct((2, 2, LINES, HA...]
    reduce_sum x2 -> x0, other arithmetic: 4.84 us -> none  [the longest x1 4.71 us: shards(): totals = jnp.sum(counts, axis=0)]
where the time goes in v2:
time: 231 us; the launch traced here: 230 us
  Pallas kernels  230 us (100%)
    pallas_call x1, Pallas kernels, shards(): pl.pallas_call(exchange, out_shape=(jax.ShapeDtypeStruct((2, 2, LINES, HA...  205 us
    pallas_call x1, Pallas kernels, shards(): pl.pallas_call(place, out_shape=(jax.ShapeDtypeStruct((2, LINES, WIDTH),...  25.3 us

profile of v2, /device:TPU:1, one launch (start us, length us, event | category | flops | bytes accessed | tf_op | source)
XLA Modules:
  0.0 230.5 jit_solution(13876466460048382826)
XLA Ops:
  0.6 204.5 %exchange.1 = (bf16[2,2,768,3584]{3,2,1,0:T(8,128)(2,1)}, s32[16,256]{1,0:T(8,128)}, s32[16,128]{1,0:T(8,128)}) custom-call(bf16[128,7168]{1,0:T(8,128)(2,1)} %tok.1, s32[8,128]{1,0:T(8,128)} %bitcast.1), custom_call_target="tpu_custom_call" | custom-call | tf_op jit(solution)/shard_map/exchange/pallas_call | solution.py:406
  205.1 25.3 %place.1 = (bf16[2,768,7168]{2,1,0:T(8,128)(2,1)}, s32[2]{0:T(128)}) custom-call(s32[16,128]{1,0:T(8,128)} %get-tuple-element.5.starts, s32[16,256]{1,0:T(8,128)} %get-tuple-element.6.goal, bf16[2,2,768,3584]{3,2,1,0:T(8,128)(2,1)} %get-tuple-element.7.rows), custom_call_target="tpu_custom_call" | custom-call | tf_op jit(solution)/shard_map/place/pallas_call | solution.py:444

commit v3 on v2

--- a/solution.py
+++ b/solution.py
@@ -40,9 +40,10 @@
     return value + flag * (flipped - value)
 
 
-def exchange(tok, ids, out, goal, starts, xg, oh, sb, mk, rk, idr, cts, ctr,
-             load_sem, swap_send, swap_recv, id_sem, id_send, id_recv, ag_send, ag_recv,
-             count_send, count_recv, put_send, put_recv, keep_sem):
+def exchange(tok, ids, out, goal, starts, xg, oh, sb, via, onward, mk, rk, idr, cts, ctr,
+             load_sem, swap_send, swap_recv, id_sem, id_send, id_recv, own_send, own_recv,
+             ag_send, ag_recv, count_send, count_recv, via_send, via_recv, onward_send,
+             onward_recv, put_send, put_recv, keep_sem):
     me = lax.axis_index("ep")
     core, x, z, y = me % 2, (me // 2) % 4, (me // 8) % 4, me // 32
 
@@ -92,20 +93,6 @@
         )
         copy.start()
         swaps.append(copy)
-    names_sent = []
-    for d in range(1, 16):
-        for h in range(2):
-            copy = pltpu.make_async_remote_copy(
-                src_ref=ids,
-                dst_ref=idr.at[h, d],
-                send_sem=id_send.at[h, d],
-                recv_sem=id_recv.at[h, d],
-                device_id=(target(SHARE[h], d),),
-                device_id_type=MESH,
-            )
-            copy.start()
-            names_sent.append(copy)
-
     def neighbour(h, bit):
         flip = SHARE[h]
         if bit == 1:
@@ -122,6 +109,19 @@
             send_sem=ag_send.at[h, n, i, slot ^ bit],
             recv_sem=ag_recv.at[h, n, i, slot ^ bit],
             device_id=(neighbour(h, bit),),
+            device_id_type=MESH,
+        )
+
+    def spread_own(h, n, i, other):
+        at, size = SPLITS[n][i]
+        cc = 1 - core if other else core
+        bit = (1, 2, 4)[i]
+        return pltpu.make_async_remote_copy(
+            src_ref=tok.at[:, pl.ds(pl.multiple_of(h * HALF + cc * QUARTER + at, 128), size)],
+            dst_ref=xg.at[h, bit, pl.ds(pl.multiple_of(core * TOK, TOK), TOK), pl.ds(at, size)],
+            send_sem=own_send.at[h, n, i, other],
+            recv_sem=own_recv.at[h, n, i, other],
+            device_id=(neighbour(h, bit) + cc - core,),
             device_id_type=MESH,
         )
 
@@ -134,7 +134,10 @@
                 held += [s ^ bits[k] for s in held]
             for slot in held:
                 for h in range(2):
-                    copies.append(spread(h, n, i, slot, bits[step]))
+                    if step == 0:
+                        copies += [spread_own(h, n, i, other) for other in range(2)]
+                    else:
+                        copies.append(spread(h, n, i, slot, bits[step]))
         return copies
 
     sub = lax.broadcasted_iota(jnp.int32, (16, TOK), 0) % 8
@@ -205,15 +208,30 @@
 
         lax.fori_loop(0, 16, places, 0)
 
+    first = [spread_step(n, 0) for n in range(2)]
+    for copy in first[0]:
+        copy.start()
+    names_sent = []
+    for d in range(1, 16):
+        for h in range(2):
+            copy = pltpu.make_async_remote_copy(
+                src_ref=ids,
+                dst_ref=idr.at[h, d],
+                send_sem=id_send.at[h, d],
+                recv_sem=id_recv.at[h, d],
+                device_id=(target(SHARE[h], d),),
+                device_id_type=MESH,
+            )
+            copy.start()
+            names_sent.append(copy)
+
+    for copy in first[1]:
+        copy.start()
     cts[...] = jnp.zeros(cts.shape, jnp.float32)
     for copy in loads:
         copy.wait()
     for copy in swaps:
         copy.wait_recv()
-    first = [spread_step(n, 0) for n in range(2)]
-    for n in range(2):
-        for copy in first[n]:
-            copy.start()
     for copy in names_sent:
         copy.wait_recv()
     build(0, 0)
@@ -249,69 +267,125 @@
     build(1, 0)
     build(1, 1)
 
-    def put(h, n, w, d):
-        ys, where = group_row(h, w // 4)
+    def shift(h, bits):
+        flip = CROSS[h]
         return (
-            sb.at[h, n, w // 4, d],
-            out.at[
-                h,
-                :,
-                pl.ds(pl.multiple_of(ys * 192 + where * 48, 16), 48),
-                pl.ds(pl.multiple_of(core * QUARTER + n * PIECE, 128), PIECE),
-            ],
-        )
-
-    def remote(h, n, w, d):
-        src, dst = put(h, n, w, d)
+            flip(y) if bits & 4 else y,
+            flip(z) if bits & 2 else z,
+            flip(x) if bits & 1 else x,
+        )
+
+    def landing(h, n, g, done):
+        yy, zz, xx = shift(h, done)
+        ys = SHARE[h](yy) if g else yy
+        where = PAIR[h](zz) * 2 + PAIR[h](xx)
+        return out.at[
+            h,
+            :,
+            pl.ds(pl.multiple_of(ys * 192 + where * 48, 16), 48),
+            pl.ds(pl.multiple_of(core * QUARTER + n * PIECE, 128), PIECE),
+        ]
+
+    def route(n, g):
+        return [(1, 2, 4)[(n * 2 + g + k) % 3] for k in range(3)]
+
+    def last_hop(h, n, g, cross, other):
+        a, b, c = route(n, g)
+        chunk = n * 2 + g
+        bit = {a: a, b: b, a | b: b}.get(cross, 0 if cross == 0 else c)
+        done = cross ^ bit
+        if done == 0:
+            src = sb.at[h, n, g, cross * 2 + other]
+        elif done == a:
+            src = via.at[h, chunk, 0 if cross == a | b else 1, other]
+        else:
+            src = onward.at[h, chunk, 0 if done == b else 1, other]
         return pltpu.make_async_remote_copy(
             src_ref=src,
-            dst_ref=dst,
-            send_sem=put_send.at[h, n, w // 4, d],
-            recv_sem=put_recv.at[h, n, w // 4, d],
-            device_id=(target(CROSS[h], d),),
-            device_id_type=MESH,
-        )
-
-    def local(h, n, w):
-        src, dst = put(h, n, w, 0)
-        return pltpu.make_async_copy(src, dst, keep_sem.at[h, n, w // 4])
-
-    def send(h, n, w):
-        for q in range(3, -1, -1):
-            d = (3 - w % 4) * 4 + q
-            if q == 0:
-                @pl.when(w % 4 == 3)
-                def _():
-                    local(h, n, w).start()
-
-                @pl.when(w % 4 != 3)
-                def _():
-                    remote(h, n, w, d).start()
-            else:
-                remote(h, n, w, d).start()
-
-    for n in range(2):
-        for copy in third[n]:
-            copy.wait_recv()
-
-        def pack(w, carry, n=n):
-            g, m = w // 4, 3 - w % 4
-            for h in range(2):
-                placer = oh[h, g, pl.ds(m * 4, 4)].reshape(384, 1024)
-                rows = xg[h, pl.ds(g * 4, 4), :, n * PIECE : (n + 1) * PIECE]
-                packed = jnp.dot(
-                    placer, rows.reshape(1024, PIECE), preferred_element_type=jnp.float32
-                )
-                sb[h, n, g, pl.ds(m * 4, 4)] = packed.astype(jnp.bfloat16).reshape(4, 2, 48, PIECE)
-
-                @pl.when(w > 0)
-                def _():
-                    send(h, n, w - 1)
+            dst_ref=landing(h, n, g, done),
+            send_sem=put_send.at[h, chunk, cross * 2 + other],
+            recv_sem=put_recv.at[h, chunk, cross * 2 + other],
+            device_id=(device(*shift(h, bit), 1 - core if other else core),),
+            device_id_type=MESH,
+        )
+
+    def first_hop(h, n, g, which):
+        a, b, c = route(n, g)
+        cross = (a | b, a | c, a | b | c)[which]
+        return pltpu.make_async_remote_copy(
+            src_ref=sb.at[h, n, g, pl.ds(cross * 2, 2)],
+            dst_ref=via.at[h, n * 2 + g, which],
+            send_sem=via_send.at[h, n * 2 + g, which],
+            recv_sem=via_recv.at[h, n * 2 + g, which],
+            device_id=(device(*shift(h, a), core),),
+            device_id_type=MESH,
+        )
+
+    def next_hop(h, n, g, which):
+        a, b, c = route(n, g)
+        chunk = n * 2 + g
+        return pltpu.make_async_remote_copy(
+            src_ref=sb.at[h, n, g, pl.ds((b | c) * 2, 2)] if which == 0 else via.at[h, chunk, 2],
+            dst_ref=onward.at[h, chunk, which],
+            send_sem=onward_send.at[h, chunk, which],
+            recv_sem=onward_recv.at[h, chunk, which],
+            device_id=(device(*shift(h, b), core),),
+            device_id_type=MESH,
+        )
+
+    def keep(h, n, g):
+        return pltpu.make_async_copy(
+            sb.at[h, n, g, 0], landing(h, n, g, 0), keep_sem.at[h, n * 2 + g]
+        )
+
+    def pack(h, n, g):
+        def some(m, carry):
+            placer = oh[h, g, pl.ds(m * 4, 4)].reshape(384, 1024)
+            rows = xg[h, g * 4 : g * 4 + 4, :, n * PIECE : (n + 1) * PIECE]
+            packed = jnp.dot(placer, rows.reshape(1024, PIECE), preferred_element_type=jnp.float32)
+            sb[h, n, g, pl.ds(m * 4, 4)] = packed.astype(jnp.bfloat16).reshape(4, 2, 48, PIECE)
             return carry
 
-        lax.fori_loop(0, 8, pack, 0)
-        for h in range(2):
-            send(h, n, 7)
+        lax.fori_loop(0, 4, some, 0)
+
+    def leave(h, n, g):
+        for which in (2, 0, 1):
+            first_hop(h, n, g, which).start()
+        next_hop(h, n, g, 0).start()
+        keep(h, n, g).start()
+        last_hop(h, n, g, 0, 1).start()
+
+    def relay(h, n, g):
+        a, b, c = route(n, g)
+        first_hop(h, n, g, 2).wait_recv()
+        next_hop(h, n, g, 1).start()
+        for which, cross in ((0, a | b), (1, a | c)):
+            first_hop(h, n, g, which).wait_recv()
+            for other in range(2):
+                last_hop(h, n, g, cross, other).start()
+        for cross in (a, b, c):
+            for other in range(2):
+                last_hop(h, n, g, cross, other).start()
+
+    def finish(h, n, g):
+        a, b, c = route(n, g)
+        for which, cross in ((0, b | c), (1, a | b | c)):
+            next_hop(h, n, g, which).wait_recv()
+            for other in range(2):
+                last_hop(h, n, g, cross, other).start()
+
+    units = [(h, n, g) for n in range(2) for g in range(2) for h in range(2)]
+    for i, (h, n, g) in enumerate(units):
+        if i % 4 == 0:
+            for copy in third[n]:
+                copy.wait_recv()
+        pack(h, n, g)
+        if i > 0:
+            leave(*units[i - 1])
+    relay(*units[0])
+    leave(*units[-1])
+    for unit in units[1:]:
+        relay(*unit)
 
     own_count.wait()
     for copy in counts:
@@ -354,50 +428,71 @@
             sums[e * 32 : e * 32 + 1, :] + sums[64 + e * 32 : 65 + e * 32, :]
         ).astype(jnp.int32)
 
+    for unit in units:
+        finish(*unit)
+
     for copy in names_sent + counts + swaps:
         copy.wait_send()
     for step in (first, second, third):
         for n in range(2):
             for copy in step[n]:
                 copy.wait_send()
-
-    for n in range(2):
-
-        def drain(g, carry, n=n):
-            for h in range(2):
-                local(h, n, g * 4).wait()
-
-                def one(d, inner, h=h):
-                    remote(h, n, g * 4, d).wait()
-                    return inner
-
-                lax.fori_loop(1, 16, one, 0)
-            return carry
-
-        lax.fori_loop(0, 2, drain, 0)
-
-
-def place(starts, goal, rows, out, totals, placer):
-    e, h, n = pl.program_id(0), pl.program_id(1), pl.program_id(2)
-
-    def window(yy):
-        return pl.multiple_of(jnp.minimum(starts[e * 4 + yy, 0] // 16 * 16, LINES - WINDOW), 16)
-
-    @pl.when(n == 0)
-    def _():
+    for unit in units:
+        for which in range(3):
+            first_hop(*unit, which).wait_send()
+        for which in range(2):
+            next_hop(*unit, which).wait_send()
+        keep(*unit).wait()
+        for cross in range(8):
+            for other in range(2):
+                if cross or other:
+                    last_hop(*unit, cross, other).wait()
+
+
+def place(starts, goal, rows, out, totals, placer, got, made, in_sem, out_sem):
+    steps = [(e, h, n) for e in range(2) for h in range(2) for n in range(4)]
+    ins = [
+        pltpu.make_async_copy(
+            rows.at[h, e, :, n * PIECE : (n + 1) * PIECE], got.at[i], in_sem.at[i]
+        )
+        for i, (e, h, n) in enumerate(steps)
+    ]
+    outs = [
+        pltpu.make_async_copy(
+            made.at[i], out.at[e, :, pl.ds(h * HALF + n * PIECE, PIECE)], out_sem.at[i]
+        )
+        for i, (e, h, n) in enumerate(steps)
+    ]
+    for copy in ins:
+        copy.start()
+    line = lax.broadcasted_iota(jnp.int32, (WINDOW, 192), 0)
+    for e in range(2):
         totals[e] = starts[8 + e, 0]
-        line = lax.broadcasted_iota(jnp.int32, (WINDOW, 192), 0)
+    for i, (e, h, n) in enumerate(steps):
+        windows = [
+            pl.multiple_of(jnp.minimum(starts[e * 4 + yy, 0] // 16 * 16, LINES - WINDOW), 16)
+            for yy in range(4)
+        ]
+        if n == 0:
+            for yy in range(4):
+                mine = (h * 2 + e) * 4 + yy
+                wanted = goal[mine : mine + 1, 0:192] - windows[yy]
+                placer[yy] = jnp.where(wanted == line, 1.0, 0.0).astype(jnp.bfloat16)
+        made[i, 192:] = jnp.zeros((LINES - 192, PIECE), jnp.bfloat16)
+        ins[i].wait()
         for yy in range(4):
-            wanted = goal[pl.ds((h * 2 + e) * 4 + yy, 1), 0:192] - window(yy)
-            placer[yy] = jnp.where(wanted == line, 1.0, 0.0).astype(jnp.bfloat16)
-
-    out[...] = jnp.zeros(out.shape, jnp.bfloat16)
-    for yy in range(4):
-        part = jnp.dot(
-            placer[yy], rows[0, 0, yy * 192 : (yy + 1) * 192, :], preferred_element_type=jnp.float32
-        ).astype(jnp.bfloat16)
-        span = pl.ds(window(yy), WINDOW)
-        out[0, span, :] = out[0, span, :] + part
+            part = jnp.dot(
+                placer[yy], got[i, yy * 192 : (yy + 1) * 192, :], preferred_element_type=jnp.float32
+            ).astype(jnp.bfloat16)
+            if yy == 0:
+                made[i, 0:WINDOW, :] = part
+            else:
+                shared = pl.ds(windows[yy], 16)
+                made[i, shared, :] = made[i, shared, :] + part[:16]
+                made[i, pl.ds(pl.multiple_of(windows[yy] + 16, 16), WINDOW - 16), :] = part[16:]
+        outs[i].start()
+    for copy in outs:
+        copy.wait()
 
 
 def shards(tokens, expert_ids):
@@ -416,6 +511,8 @@
             pltpu.VMEM((2, 8, 2 * TOK, QUARTER), jnp.bfloat16),
             pltpu.VMEM((2, 2, 16, 96, 8 * TOK), jnp.bfloat16),
             pltpu.VMEM((2, 2, 2, 16, 2, 48, PIECE), jnp.bfloat16),
+            pltpu.VMEM((2, 4, 3, 2, 2, 48, PIECE), jnp.bfloat16),
+            pltpu.VMEM((2, 4, 2, 2, 2, 48, PIECE), jnp.bfloat16),
             pltpu.VMEM((256, TOK), jnp.float32),
             pltpu.VMEM((256, TOK), jnp.float32),
             pltpu.VMEM((2, 16, TOP, TOK), jnp.int32),
@@ -427,16 +524,22 @@
             pltpu.SemaphoreType.DMA((2,)),
             pltpu.SemaphoreType.DMA((2, 16)),
             pltpu.SemaphoreType.DMA((2, 16)),
+            pltpu.SemaphoreType.DMA((2, 2, 3, 2)),
+            pltpu.SemaphoreType.DMA((2, 2, 3, 2)),
             pltpu.SemaphoreType.DMA((2, 2, 3, 8)),
             pltpu.SemaphoreType.DMA((2, 2, 3, 8)),
             pltpu.SemaphoreType.DMA((8,)),
             pltpu.SemaphoreType.DMA((8,)),
-            pltpu.SemaphoreType.DMA((2, 2, 2, 16)),
-            pltpu.SemaphoreType.DMA((2, 2, 2, 16)),
-            pltpu.SemaphoreType.DMA((2, 2, 2)),
+            pltpu.SemaphoreType.DMA((2, 4, 3)),
+            pltpu.SemaphoreType.DMA((2, 4, 3)),
+            pltpu.SemaphoreType.DMA((2, 4, 2)),
+            pltpu.SemaphoreType.DMA((2, 4, 2)),
+            pltpu.SemaphoreType.DMA((2, 4, 16)),
+            pltpu.SemaphoreType.DMA((2, 4, 16)),
+            pltpu.SemaphoreType.DMA((2, 4)),
         ],
         compiler_params=pltpu.CompilerParams(
-            collective_id=0, has_side_effects=True, vmem_limit_bytes=62 * 1024 * 1024
+            collective_id=0, has_side_effects=True, vmem_limit_bytes=67043328
         ),
         name="exchange",
     )(tokens, expert_ids.T)
@@ -447,17 +550,16 @@
             jax.ShapeDtypeStruct((2, LINES, WIDTH), jnp.bfloat16),
             jax.ShapeDtypeStruct((2,), jnp.int32),
         ),
-        grid=(2, 2, 4),
-        in_specs=[
-            pl.BlockSpec(memory_space=pltpu.SMEM),
-            vmem,
-            pl.BlockSpec((1, 1, LINES, HALF // 4), lambda e, h, n: (h, e, 0, n)),
+        in_specs=[pl.BlockSpec(memory_space=pltpu.SMEM), vmem, anywhere],
+        out_specs=(anywhere, pl.BlockSpec(memory_space=pltpu.SMEM)),
+        scratch_shapes=[
+            pltpu.VMEM((4, WINDOW, 192), jnp.bfloat16),
+            pltpu.VMEM((16, LINES, PIECE), jnp.bfloat16),
+            pltpu.VMEM((16, LINES, PIECE), jnp.bfloat16),
+            pltpu.SemaphoreType.DMA((16,)),
+            pltpu.SemaphoreType.DMA((16,)),
         ],
-        out_specs=(
-            pl.BlockSpec((1, LINES, HALF // 4), lambda e, h, n: (e, 0, h * 4 + n)),
-            pl.BlockSpec(memory_space=pltpu.SMEM),
-        ),
-        scratch_shapes=[pltpu.VMEM((4, WINDOW, 192), jnp.bfloat16)],
+        compiler_params=pltpu.CompilerParams(vmem_limit_bytes=60 * 1024 * 1024),
         name="place",
     )(starts, goal, arrived)
 

time: 231 us -> 217 us (0.939)
  Pallas kernels: 230 us -> 216 us
    pallas_call x1, Pallas kernels: 25.3 us -> 17 us  [shards(): pl.pallas_call(place, out_shape=(jax.ShapeDtypeStruct((2, LINES, WIDTH),...]
    pallas_call x1, Pallas kernels: 205 us -> 199 us  [shards(): pl.pallas_call(exchange, out_shape=(jax.ShapeDtypeStruct((2, 2, LINES, HA...]
where the time goes in v3:
time: 217 us; the launch traced here: 216 us
  Pallas kernels  216 us (100%)
    pallas_call x1, Pallas kernels, shards(): pl.pallas_call(exchange, out_shape=(jax.ShapeDtypeStruct((2, 2, LINES, HA...  199 us
    pallas_call x1, Pallas kernels, shards(): pl.pallas_call(place, out_shape=(jax.ShapeDtypeStruct((2, LINES, WIDTH),...  17 us

profile of v3, /device:TPU:1, one launch (start us, length us, event | category | flops | bytes accessed | tf_op | source)
XLA Modules:
  0.0 216.4 jit_solution(6660908959500624832)
XLA Ops:
  0.6 198.6 %exchange.1 = (bf16[2,2,768,3584]{3,2,1,0:T(8,128)(2,1)}, s32[16,256]{1,0:T(8,128)}, s32[16,128]{1,0:T(8,128)}) custom-call(bf16[128,7168]{1,0:T(8,128)(2,1)} %tok.1, s32[8,128]{1,0:T(8,128)} %bitcast.1), custom_call_target="tpu_custom_call" | custom-call | tf_op jit(solution)/shard_map/exchange/pallas_call | solution.py:501
  199.2 17.0 %place.1 = (bf16[2,768,7168]{2,1,0:T(8,128)(2,1)}, s32[2]{0:T(128)}) custom-call(s32[16,128]{1,0:T(8,128)} %get-tuple-element.5.starts, s32[16,256]{1,0:T(8,128)} %get-tuple-element.6.goal, bf16[2,2,768,3584]{3,2,1,0:T(8,128)(2,1)} %get-tuple-element.7.rows), custom_call_target="tpu_custom_call" | custom-call | tf_op jit(solution)/shard_map/place/pallas_call | solution.py:547

commit v4 on v3

--- a/solution.py
+++ b/solution.py
@@ -19,6 +19,7 @@
 SPLITS = (((0, 384), (384, 256), (640, 256)), ((896, 256), (1152, 384), (1536, 256)))
 MESH = pl.DeviceIdType.MESH
 WINDOW = 208
+ROUTES = ((1, 2, 4), (4, 2, 1), (1, 4, 2), (2, 1, 4))
 
 
 def near(v):
@@ -40,10 +41,10 @@
     return value + flag * (flipped - value)
 
 
-def exchange(tok, ids, out, goal, starts, xg, oh, sb, via, onward, mk, rk, idr, cts, ctr,
+def exchange(tok, ids, out, goal, starts, shared, via, onward, xg, oh, sb, mk, rk, idr, cts, ctr,
              load_sem, swap_send, swap_recv, id_sem, id_send, id_recv, own_send, own_recv,
-             ag_send, ag_recv, count_send, count_recv, via_send, via_recv, onward_send,
-             onward_recv, put_send, put_recv, keep_sem):
+             pass_send, pass_recv, count_send, count_recv, via_send, via_recv, onward_send,
+             onward_recv, put_send, put_recv, keep_sem, fetch_sem):
     me = lax.axis_index("ep")
     core, x, z, y = me % 2, (me // 2) % 4, (me // 8) % 4, me // 32
 
@@ -101,44 +102,64 @@
             return device(y, flip(z), x, core)
         return device(flip(y), z, x, core)
 
-    def spread(h, n, i, slot, bit):
+    def turns(i):
+        return [(1, 2, 4)[(i + k) % 3] for k in range(3)]
+
+    def give(h, n, i, step, other):
         at, size = SPLITS[n][i]
+        cc = 1 - core if other else core
+        bit = turns(i)[step]
         return pltpu.make_async_remote_copy(
-            src_ref=xg.at[h, slot, :, pl.ds(at, size)],
-            dst_ref=xg.at[h, slot ^ bit, :, pl.ds(at, size)],
-            send_sem=ag_send.at[h, n, i, slot ^ bit],
-            recv_sem=ag_recv.at[h, n, i, slot ^ bit],
+            src_ref=tok.at[:, pl.ds(pl.multiple_of(h * HALF + cc * QUARTER + at, 128), size)],
+            dst_ref=shared.at[h, bit, pl.ds(pl.multiple_of(core * TOK, TOK), TOK), pl.ds(at, size)],
+            send_sem=own_send.at[h, n, i, step, other],
+            recv_sem=own_recv.at[h, n, i, step, other],
+            device_id=(neighbour(h, bit) + cc - core,),
+            device_id_type=MESH,
+        )
+
+    def pass_on(h, n, i, kind):
+        at, size = SPLITS[n][i]
+        a, b, c = turns(i)
+        slot, bit = ((a, b), (a, c), (b, c), (a | b, c))[kind]
+        return pltpu.make_async_remote_copy(
+            src_ref=shared.at[h, slot, :, pl.ds(at, size)],
+            dst_ref=shared.at[h, slot | bit, :, pl.ds(at, size)],
+            send_sem=pass_send.at[h, n, i, kind],
+            recv_sem=pass_recv.at[h, n, i, kind],
             device_id=(neighbour(h, bit),),
             device_id_type=MESH,
         )
 
-    def spread_own(h, n, i, other):
-        at, size = SPLITS[n][i]
-        cc = 1 - core if other else core
-        bit = (1, 2, 4)[i]
-        return pltpu.make_async_remote_copy(
-            src_ref=tok.at[:, pl.ds(pl.multiple_of(h * HALF + cc * QUARTER + at, 128), size)],
-            dst_ref=xg.at[h, bit, pl.ds(pl.multiple_of(core * TOK, TOK), TOK), pl.ds(at, size)],
-            send_sem=own_send.at[h, n, i, other],
-            recv_sem=own_recv.at[h, n, i, other],
-            device_id=(neighbour(h, bit) + cc - core,),
-            device_id_type=MESH,
-        )
-
-    def spread_step(n, step):
-        copies = []
-        for i in range(3):
-            bits = [(1, 2, 4)[(i + k) % 3] for k in range(3)]
-            held = [0]
-            for k in range(step):
-                held += [s ^ bits[k] for s in held]
-            for slot in held:
-                for h in range(2):
-                    if step == 0:
-                        copies += [spread_own(h, n, i, other) for other in range(2)]
-                    else:
-                        copies.append(spread(h, n, i, slot, bits[step]))
-        return copies
+    both = [(h, i) for i in range(3) for h in range(2)]
+
+    def give_all(n):
+        for step in range(3):
+            for h, i in both:
+                for other in range(2):
+                    give(h, n, i, step, other).start()
+
+    def took(n, step):
+        for h, i in both:
+            for other in range(2):
+                give(h, n, i, step, other).wait_recv()
+
+    def pass_all(n, kind):
+        for h, i in both:
+            pass_on(h, n, i, kind).start()
+
+    def passed(n, kind):
+        for h, i in both:
+            pass_on(h, n, i, kind).wait_recv()
+
+    def fetch(h, n, g):
+        cols = slice(n * PIECE, (n + 1) * PIECE)
+        first = 1 if g == 0 else 4
+        return pltpu.make_async_copy(
+            shared.at[h, first : g * 4 + 4, :, cols],
+            xg.at[h, first : g * 4 + 4, :, cols],
+            fetch_sem.at[h, n, g],
+        )
 
     sub = lax.broadcasted_iota(jnp.int32, (16, TOK), 0) % 8
     lane = lax.broadcasted_iota(jnp.int32, (8, TOK), 1)
@@ -208,9 +229,7 @@
 
         lax.fori_loop(0, 16, places, 0)
 
-    first = [spread_step(n, 0) for n in range(2)]
-    for copy in first[0]:
-        copy.start()
+    give_all(0)
     names_sent = []
     for d in range(1, 16):
         for h in range(2):
@@ -225,9 +244,12 @@
             copy.start()
             names_sent.append(copy)
 
-    for copy in first[1]:
-        copy.start()
     cts[...] = jnp.zeros(cts.shape, jnp.float32)
+    took(0, 0)
+    pass_all(0, 0)
+    pass_all(0, 1)
+    took(0, 1)
+    pass_all(0, 2)
     for copy in loads:
         copy.wait()
     for copy in swaps:
@@ -235,19 +257,17 @@
     for copy in names_sent:
         copy.wait_recv()
     build(0, 0)
-    second = [spread_step(n, 1) for n in range(2)]
-    for n in range(2):
-        for copy in first[n]:
-            copy.wait_recv()
-        for copy in second[n]:
-            copy.start()
+    passed(0, 0)
+    pass_all(0, 3)
+    give_all(1)
+    took(1, 0)
+    pass_all(1, 0)
+    pass_all(1, 1)
+    took(1, 1)
+    pass_all(1, 2)
     build(0, 1)
-    third = [spread_step(n, 2) for n in range(2)]
-    for n in range(2):
-        for copy in second[n]:
-            copy.wait_recv()
-        for copy in third[n]:
-            copy.start()
+    passed(1, 0)
+    pass_all(1, 3)
 
     block = (y // 2) * 4 + (z // 2) * 2 + x // 2
     counts = []
@@ -287,7 +307,7 @@
         ]
 
     def route(n, g):
-        return [(1, 2, 4)[(n * 2 + g + k) % 3] for k in range(3)]
+        return ROUTES[n * 2 + g]
 
     def last_hop(h, n, g, cross, other):
         a, b, c = route(n, g)
@@ -355,6 +375,11 @@
         keep(h, n, g).start()
         last_hop(h, n, g, 0, 1).start()
 
+    def direct(h, n, g):
+        for cross in route(n, g):
+            for other in range(2):
+                last_hop(h, n, g, cross, other).start()
+
     def relay(h, n, g):
         a, b, c = route(n, g)
         first_hop(h, n, g, 2).wait_recv()
@@ -363,9 +388,8 @@
             first_hop(h, n, g, which).wait_recv()
             for other in range(2):
                 last_hop(h, n, g, cross, other).start()
-        for cross in (a, b, c):
-            for other in range(2):
-                last_hop(h, n, g, cross, other).start()
+        if n == 1:
+            direct(h, n, g)
 
     def finish(h, n, g):
         a, b, c = route(n, g)
@@ -375,17 +399,23 @@
                 last_hop(h, n, g, cross, other).start()
 
     units = [(h, n, g) for n in range(2) for g in range(2) for h in range(2)]
-    for i, (h, n, g) in enumerate(units):
-        if i % 4 == 0:
-            for copy in third[n]:
-                copy.wait_recv()
+
+    def gather(n):
+        took(n, 2)
+        for kind in range(1, 4):
+            passed(n, kind)
+        for g in range(2):
+            for h in range(2):
+                fetch(h, n, g).start()
+
+    gather(0)
+    for i in range(4):
+        h, n, g = units[i]
+        fetch(h, n, g).wait()
         pack(h, n, g)
         if i > 0:
             leave(*units[i - 1])
-    relay(*units[0])
-    leave(*units[-1])
-    for unit in units[1:]:
-        relay(*unit)
+            direct(*units[i - 1])
 
     own_count.wait()
     for copy in counts:
@@ -428,15 +458,36 @@
             sums[e * 32 : e * 32 + 1, :] + sums[64 + e * 32 : 65 + e * 32, :]
         ).astype(jnp.int32)
 
-    for unit in units:
-        finish(*unit)
+    leave(*units[3])
+    direct(*units[3])
+    gather(1)
+    for i in range(4, 8):
+        h, n, g = units[i]
+        fetch(h, n, g).wait()
+        pack(h, n, g)
+        if i > 4:
+            leave(*units[i - 1])
+        relay(*units[i - 4])
+    finish(*units[0])
+    leave(*units[7])
+    finish(*units[1])
+    for at in (4, 6):
+        relay(*units[at])
+        relay(*units[at + 1])
+        finish(*units[at - 2])
+        finish(*units[at - 1])
+    finish(*units[6])
+    finish(*units[7])
 
     for copy in names_sent + counts + swaps:
         copy.wait_send()
-    for step in (first, second, third):
-        for n in range(2):
-            for copy in step[n]:
-                copy.wait_send()
+    for n in range(2):
+        for h, i in both:
+            for step in range(3):
+                for other in range(2):
+                    give(h, n, i, step, other).wait_send()
+            for kind in range(4):
+                pass_on(h, n, i, kind).wait_send()
     for unit in units:
         for which in range(3):
             first_hop(*unit, which).wait_send()
@@ -498,21 +549,22 @@
 def shards(tokens, expert_ids):
     anywhere = pl.BlockSpec(memory_space=pl.ANY)
     vmem = pl.BlockSpec(memory_space=pltpu.VMEM)
-    arrived, goal, starts = pl.pallas_call(
+    arrived, goal, starts, *_ = pl.pallas_call(
         exchange,
         out_shape=(
             jax.ShapeDtypeStruct((2, 2, LINES, HALF), jnp.bfloat16),
             jax.ShapeDtypeStruct((16, 256), jnp.int32),
             jax.ShapeDtypeStruct((16, TOK), jnp.int32),
+            jax.ShapeDtypeStruct((2, 8, 2 * TOK, QUARTER), jnp.bfloat16),
+            jax.ShapeDtypeStruct((2, 4, 3, 2, 2, 48, PIECE), jnp.bfloat16),
+            jax.ShapeDtypeStruct((2, 4, 2, 2, 2, 48, PIECE), jnp.bfloat16),
         ),
         in_specs=[anywhere, vmem],
-        out_specs=(anywhere, vmem, vmem),
+        out_specs=(anywhere, vmem, vmem, anywhere, anywhere, anywhere),
         scratch_shapes=[
             pltpu.VMEM((2, 8, 2 * TOK, QUARTER), jnp.bfloat16),
             pltpu.VMEM((2, 2, 16, 96, 8 * TOK), jnp.bfloat16),
             pltpu.VMEM((2, 2, 2, 16, 2, 48, PIECE), jnp.bfloat16),
-            pltpu.VMEM((2, 4, 3, 2, 2, 48, PIECE), jnp.bfloat16),
-            pltpu.VMEM((2, 4, 2, 2, 2, 48, PIECE), jnp.bfloat16),
             pltpu.VMEM((256, TOK), jnp.float32),
             pltpu.VMEM((256, TOK), jnp.float32),
             pltpu.VMEM((2, 16, TOP, TOK), jnp.int32),
@@ -524,10 +576,10 @@
             pltpu.SemaphoreType.DMA((2,)),
             pltpu.SemaphoreType.DMA((2, 16)),
             pltpu.SemaphoreType.DMA((2, 16)),
-            pltpu.SemaphoreType.DMA((2, 2, 3, 2)),
-            pltpu.SemaphoreType.DMA((2, 2, 3, 2)),
-            pltpu.SemaphoreType.DMA((2, 2, 3, 8)),
-            pltpu.SemaphoreType.DMA((2, 2, 3, 8)),
+            pltpu.SemaphoreType.DMA((2, 2, 3, 3, 2)),
+            pltpu.SemaphoreType.DMA((2, 2, 3, 3, 2)),
+            pltpu.SemaphoreType.DMA((2, 2, 3, 4)),
+            pltpu.SemaphoreType.DMA((2, 2, 3, 4)),
             pltpu.SemaphoreType.DMA((8,)),
             pltpu.SemaphoreType.DMA((8,)),
             pltpu.SemaphoreType.DMA((2, 4, 3)),
@@ -537,9 +589,10 @@
             pltpu.SemaphoreType.DMA((2, 4, 16)),
             pltpu.SemaphoreType.DMA((2, 4, 16)),
             pltpu.SemaphoreType.DMA((2, 4)),
+            pltpu.SemaphoreType.DMA((2, 2, 2)),
         ],
         compiler_params=pltpu.CompilerParams(
-            collective_id=0, has_side_effects=True, vmem_limit_bytes=67043328
+            collective_id=0, has_side_effects=True, vmem_limit_bytes=60 * 1024 * 1024
         ),
         name="exchange",
     )(tokens, expert_ids.T)

time: 217 us -> 213 us (0.982)
  Pallas kernels: 216 us -> 212 us
    pallas_call x1, Pallas kernels: 199 us -> 195 us  [shards(): pl.pallas_call(exchange, out_shape=(jax.ShapeDtypeStruct((2, 2, LINES, HA...]
where the time goes in v4:
time: 213 us
  Pallas kernels  212 us (100%)
    pallas_call x1, Pallas kernels, shards(): pl.pallas_call(exchange, out_shape=(jax.ShapeDtypeStruct((2, 2, LINES, HA...  195 us
    pallas_call x1, Pallas kernels, shards(): pl.pallas_call(place, out_shape=(jax.ShapeDtypeStruct((2, LINES, WIDTH),...  17 us

profile of v4, /device:TPU:1, one launch (start us, length us, event | category | flops | bytes accessed | tf_op | source)
XLA Modules:
  0.0 212.6 jit_solution(6481424285133531294)
XLA Ops:
  0.6 194.8 %exchange.1 = (bf16[2,2,768,3584]{3,2,1,0:T(8,128)(2,1)}, s32[16,256]{1,0:T(8,128)}, s32[16,128]{1,0:T(8,128)}, bf16[2,8,256,1792]{3,2,1,0:T(8,128)(2,1)}, bf16[...) custom-call(bf16[128,7168]{1,0:T(8,128)(2,1)} %tok.1, s32[8,128]{1,0:T(8,128)} %bitcast.1), custom_call_target="tpu_custom_call" | custom-call | tf_op jit(solution)/shard_map/exchange/pallas_call | solution.py:552
  195.4 17.0 %place.1 = (bf16[2,768,7168]{2,1,0:T(8,128)(2,1)}, s32[2]{0:T(128)}) custom-call(s32[16,128]{1,0:T(8,128)} %get-tuple-element.5.starts, s32[16,256]{1,0:T(8,128)} %get-tuple-element.6.goal, bf16[2,2,768,3584]{3,2,1,0:T(8,128)(2,1)} %get-tuple-element.7.rows), custom_call_target="tpu_custom_call" | custom-call | tf_op jit(solution)/shard_map/place/pallas_call | solution.py:600

commit v5 on v4

--- a/solution.py
+++ b/solution.py
@@ -254,12 +254,12 @@
         copy.wait()
     for copy in swaps:
         copy.wait_recv()
+    passed(0, 0)
+    pass_all(0, 3)
+    give_all(1)
     for copy in names_sent:
         copy.wait_recv()
     build(0, 0)
-    passed(0, 0)
-    pass_all(0, 3)
-    give_all(1)
     took(1, 0)
     pass_all(1, 0)
     pass_all(1, 1)
@@ -417,6 +417,19 @@
             leave(*units[i - 1])
             direct(*units[i - 1])
 
+    leave(*units[3])
+    direct(*units[3])
+    gather(1)
+    for i in range(4, 8):
+        h, n, g = units[i]
+        fetch(h, n, g).wait()
+        pack(h, n, g)
+        if i > 4:
+            leave(*units[i - 1])
+        relay(*units[i - 4])
+    finish(*units[0])
+    leave(*units[7])
+    finish(*units[1])
     own_count.wait()
     for copy in counts:
         copy.wait_recv()
@@ -458,19 +471,6 @@
             sums[e * 32 : e * 32 + 1, :] + sums[64 + e * 32 : 65 + e * 32, :]
         ).astype(jnp.int32)
 
-    leave(*units[3])
-    direct(*units[3])
-    gather(1)
-    for i in range(4, 8):
-        h, n, g = units[i]
-        fetch(h, n, g).wait()
-        pack(h, n, g)
-        if i > 4:
-            leave(*units[i - 1])
-        relay(*units[i - 4])
-    finish(*units[0])
-    leave(*units[7])
-    finish(*units[1])
     for at in (4, 6):
         relay(*units[at])
         relay(*units[at + 1])

time: 213 us -> 213 us (level)
  no operation moved by 1% of the time
where the time goes in v5:
time: 213 us
  Pallas kernels  212 us (100%)
    pallas_call x1, Pallas kernels, shards(): pl.pallas_call(exchange, out_shape=(jax.ShapeDtypeStruct((2, 2, LINES, HA...  195 us
    pallas_call x1, Pallas kernels, shards(): pl.pallas_call(place, out_shape=(jax.ShapeDtypeStruct((2, LINES, WIDTH),...  17 us

profile of v5, /device:TPU:1, one launch (start us, length us, event | category | flops | bytes accessed | tf_op | source)
XLA Modules:
  0.0 212.6 jit_solution(17391995775652251752)
XLA Ops:
  0.6 194.8 %exchange.1 = (bf16[2,2,768,3584]{3,2,1,0:T(8,128)(2,1)}, s32[16,256]{1,0:T(8,128)}, s32[16,128]{1,0:T(8,128)}, bf16[2,8,256,1792]{3,2,1,0:T(8,128)(2,1)}, bf16[...) custom-call(bf16[128,7168]{1,0:T(8,128)(2,1)} %tok.1, s32[8,128]{1,0:T(8,128)} %bitcast.1), custom_call_target="tpu_custom_call" | custom-call | tf_op jit(solution)/shard_map/exchange/pallas_call | solution.py:552
  195.4 17.0 %place.1 = (bf16[2,768,7168]{2,1,0:T(8,128)(2,1)}, s32[2]{0:T(128)}) custom-call(s32[16,128]{1,0:T(8,128)} %get-tuple-element.5.starts, s32[16,256]{1,0:T(8,128)} %get-tuple-element.6.goal, bf16[2,2,768,3584]{3,2,1,0:T(8,128)(2,1)} %get-tuple-element.7.rows), custom_call_target="tpu_custom_call" | custom-call | tf_op jit(solution)/shard_map/place/pallas_call | solution.py:600
